TPU v7x, 32 devices: a whole 2x2x4 slice. The times are simulated.
32 devices in a mesh: gx: 4 (over x, core), gy: 4 (over z), gz: 2 (over y).
Axes of the slice: x: 2, y: 2, z: 4, core: 2. Of those that a mesh axis runs over, the one named last changes fastest.
Arguments:
- orbitals: float32 [16, 32, 32, 512], P(None, 'gx', 'gy', 'gz'), may hold values from -10 to 10
- potential: float32 [32, 32, 512], P('gx', 'gy', 'gz'), may hold values from 0 to 12
Outputs:
- updated: float32 [16, 32, 32, 512], P(None, 'gx', 'gy', 'gz')
- trial_energies: float32 [16], replicated
All inputs are finite; a program needn't handle non-finite values.
Results may differ from a plain program's by a relative error of at most 0.000022.
Values sent between devices are 32-bit elements; how exact they have to be, the bound alone decides.
A program may use at most 64 MiB of HBM per device.

v0:
```python
import jax
import jax.numpy as jnp
from jax import lax
from jax.sharding import PartitionSpec as P

COARSE_SWEEPS = 4
CENTRE_COEF = -2.5
NEAR_COEF = 4.0 / 3.0
FAR_COEF = -1.0 / 12.0
WEIGHT = 0.8
FINE_DIAG = 4.0
COARSE_DIAG = 1.75
EPSILON = 1e-06


def with_halo(block, sides, width):
    for axis, dim in sides:
        count = lax.axis_size(axis)
        forward = [(i, i + 1) for i in range(count - 1)]
        forward.append((count - 1, 0))
        backward = [(target, source) for source, target in forward]
        low = lax.ppermute(
            lax.slice_in_dim(block, block.shape[dim] - width, None, axis=dim), axis, forward
        )
        high = lax.ppermute(lax.slice_in_dim(block, 0, width, axis=dim), axis, backward)
        block = jnp.concatenate([low, block, high], axis=dim)
    return block


def neighbor(padded, margin, dimension, offset, extent):
    starts = [0, margin, margin, margin]
    starts[dimension] = margin + offset
    limits = [opening + length for opening, length in zip(starts, extent)]
    return lax.slice(padded, starts, limits)


def hamiltonian(values, potential):
    padded = with_halo(values, (("gx", 1), ("gy", 2), ("gz", 3)), 2)
    summed = 3.0 * CENTRE_COEF * values
    for dimension in (1, 2, 3):
        summed = summed + NEAR_COEF * (
            neighbor(padded, 2, dimension, -1, values.shape)
            + neighbor(padded, 2, dimension, 1, values.shape)
        )
        summed = summed + FAR_COEF * (
            neighbor(padded, 2, dimension, -2, values.shape)
            + neighbor(padded, 2, dimension, 2, values.shape)
        )
    return -0.5 * summed + potential[None] * values


def around_cells(padded, extent):
    beside_all = jnp.zeros(extent, jnp.float32)
    for dimension in (1, 2, 3):
        beside_all = (
            beside_all
            + neighbor(padded, 1, dimension, -1, extent)
            + neighbor(padded, 1, dimension, 1, extent)
        )
    return beside_all


def fine_operator(values):
    padded = with_halo(values, (("gx", 1), ("gy", 2), ("gz", 3)), 1)
    return FINE_DIAG * values - 0.5 * around_cells(padded, values.shape)


def coarse_operator(values):
    padded = with_halo(values, (("gx", 1), ("gy", 2), ("gz", 3)), 1)
    return COARSE_DIAG * values - 0.125 * around_cells(padded, values.shape)


def precondition(residual):
    smoothed = WEIGHT * residual / FINE_DIAG
    remainder = residual - fine_operator(smoothed)
    bands, size_x, size_y, size_z = remainder.shape
    blocked = (bands, size_x // 2, 2, size_y // 2, 2, size_z // 2, 2)
    coarse_res = remainder.reshape(blocked).mean(axis=(2, 4, 6))
    approx = WEIGHT * coarse_res / COARSE_DIAG
    for sweep_index in range(COARSE_SWEEPS - 1):
        approx = approx + WEIGHT * (coarse_res - coarse_operator(approx)) / COARSE_DIAG
    lifted = jnp.broadcast_to(approx[:, :, None, :, None, :, None], blocked).reshape(
        remainder.shape
    )
    second = smoothed + lifted
    return second + WEIGHT * (residual - fine_operator(second)) / FINE_DIAG


def inner_product(left, right):
    return jnp.sum(left * right, axis=(1, 2, 3))


def expand(vector):
    return vector[:, None, None, None]


def body(orbitals, potential):
    applied = hamiltonian(orbitals, potential)
    first_sums = lax.psum(
        jnp.stack([inner_product(orbitals, orbitals), inner_product(orbitals, applied)]),
        ("gx", "gy", "gz"),
    )
    norm_orbitals = first_sums[0]
    energy = first_sums[1] / (norm_orbitals + EPSILON)
    residual = applied - expand(energy) * orbitals
    corrected = precondition(residual)
    applied_corr = hamiltonian(corrected, potential)
    response = applied_corr - expand(energy) * corrected
    correlations = lax.psum(
        jnp.stack(
            [
                inner_product(residual, response),
                inner_product(response, response),
                inner_product(orbitals, corrected),
                inner_product(corrected, corrected),
                inner_product(orbitals, applied_corr),
                inner_product(corrected, applied),
                inner_product(corrected, applied_corr),
                inner_product(residual, orbitals),
                inner_product(residual, corrected),
                inner_product(response, orbitals),
                inner_product(response, corrected),
            ]
        ),
        ("gx", "gy", "gz"),
    )
    lambda_step = -correlations[0] / (correlations[1] + EPSILON)
    trial_norm = (
        norm_orbitals
        + 2.0 * lambda_step * correlations[2]
        + lambda_step * lambda_step * correlations[3]
    )
    trial_sum = (
        first_sums[1]
        + lambda_step * (correlations[4] + correlations[5])
        + lambda_step * lambda_step * correlations[6]
    )
    trial_energies = trial_sum / (trial_norm + EPSILON)
    change = trial_energies - energy
    trial_wave = orbitals + expand(lambda_step) * corrected
    residual_change = expand(lambda_step) * response - expand(change) * trial_wave
    projected = lambda_step * correlations[0] - change * (
        correlations[7] + lambda_step * correlations[8]
    )
    cross_term = correlations[9] + lambda_step * correlations[10]
    change_norm = (
        lambda_step * lambda_step * correlations[1]
        - 2.0 * lambda_step * change * cross_term
        + change * change * trial_norm
    )
    mixing_coef = -projected / (change_norm + EPSILON)
    mixed_res = residual + expand(mixing_coef) * residual_change
    updated = (
        orbitals
        + expand(mixing_coef * lambda_step) * corrected
        + expand(lambda_step) * precondition(mixed_res)
    )
    return (updated, trial_energies)


def solution(mesh):
    return jax.shard_map(
        body,
        mesh=mesh,
        in_specs=(P(None, "gx", "gy", "gz"), P("gx", "gy", "gz")),
        out_specs=(P(None, "gx", "gy", "gz"), P()),
        check_vma=False,
    )
```

profile of v0, /device:TPU:0, one launch (start us, length us, event | category | flops | bytes accessed | tf_op | source)
XLA Modules:
  0.0 567.6 jit_solution(9485600245943928243)
XLA Ops:
  15.4 9.3 %collective-permute-done.3 = f32[16,12,2,256]{3,0,2,1:T(8,128)S(1)} collective-permute-done((f32[16,12,2,256]{3,0,2,1:T(8,128)S(1)}, f32[16,12,2,256]{3,0,2,1:T(8,128)S(1)}, u32[]{:S(2)}, u32[]{:S(2)}) %collective-permute-start.3) | collective-permute-done | bytes 393248 | tf_op jit(solution)/shard_map/ppermute | solution.py:25
  25.0 8.7 %collective-permute-done.2 = f32[16,12,2,256]{3,0,2,1:T(8,128)S(1)} collective-permute-done((f32[16,12,2,256]{3,0,2,1:T(8,128)S(1)}, f32[16,12,2,256]{3,0,2,1:T(8,128)S(1)}, u32[]{:S(2)}, u32[]{:S(2)}) %collective-permute-start.2) | collective-permute-done | bytes 393248 | tf_op jit(solution)/shard_map/ppermute | solution.py:22
  53.4 7.4 %multiply_reduce_fusion.12 = (f32[16]{0:T(128)S(1)}, f32[16]{0:T(128)S(1)}, f32[16,8,8,256]{3,2,1,0:T(8,128)}) fusion(f32[16,8,8,256]{3,2,1,0:T(8,128)S(1)} %copy-done, f32[8,8,256]{2,1,0:T(8,128)S(1)} %copy-done.17, f32[16,12,12,2]{3,2,1,0:T(8,128)} %copy.716, f32[16,12,2,256]{3,2,1,0:T(2,128)S(1)} %copy.710, f32[16,12,8,256]{3,2,1,0:T(8,128)S(1)} %get-tuple-element.88, ...), kind=kLoop, calls=%fused_computation.203 | loop fusion | flops 11010016 | bytes 8753280 | tf_op jit(solution)/shard_map/reduce_sum | solution.py:90
  60.8 39.4 %psum.14 = f32[2,16]{1,0:T(2,128)S(1)} all-reduce(f32[2,16]{1,0:T(2,128)S(1)} %pad_maximum_fusion.251), channel_id=1, replica_groups=mesh['gx'=4,'gy'=4,'gz'=2] {'gx','gy','gz'}, use_global_device_ids=true, to_apply=%region_2.0 | all-reduce | flops 32 | bytes 256 | tf_op jit(solution)/shard_map/psum | solution.py:99
  109.9 4.6 collective-permute-done.9
  138.6 6.0 %copy.727 = f32[16,8,8,256]{0,3,2,1:T(8,128)} copy(f32[16,8,8,256]{3,2,1,0:T(8,128)} %fusion.53) | data formatting | bytes 2097152 | tf_op jit(solution)/shard_map/sub | solution.py:75
  144.7 8.7 %reduce_sum.137 = f32[16,4,4,128]{0,3,2,1:T(8,128)S(1)} reduce(f32[16,4,2,4,2,128,2]{0,6,5,4,3,2,1:T(2,128)} %bitcast.133, f32[]{:T(128)} %constant.50.clone.1), dimensions={2,4,6}, to_apply=%region_3.0 | reduce | flops 229376 | bytes 1179652 | tf_op jit(solution)/shard_map/reduce_sum | solution.py:78
  165.9 7.9 %collective-permute-done.16 = f32[16,6,6,1]{3,0,2,1:T(8,128)S(1)} collective-permute-done((f32[16,6,6,1]{3,0,2,1:T(8,128)S(1)}, f32[16,6,6,1]{3,0,2,1:T(8,128)S(1)}, u32[]{:S(2)}, u32[]{:S(2)}) %collective-permute-start.16) | collective-permute-done | bytes 2336 | tf_op jit(solution)/shard_map/ppermute | solution.py:22
  173.7 5.7 %collective-permute-done.17 = f32[16,6,6,1]{3,0,2,1:T(8,128)S(1)} collective-permute-done((f32[16,6,6,1]{3,0,2,1:T(8,128)S(1)}, f32[16,6,6,1]{3,0,2,1:T(8,128)S(1)}, u32[]{:S(2)}, u32[]{:S(2)}) %collective-permute-start.17) | collective-permute-done | bytes 2336 | tf_op jit(solution)/shard_map/ppermute | solution.py:25
  192.3 7.9 %collective-permute-done.22 = f32[16,6,6,1]{3,0,2,1:T(8,128)S(1)} collective-permute-done((f32[16,6,6,1]{3,0,2,1:T(8,128)S(1)}, f32[16,6,6,1]{3,0,2,1:T(8,128)S(1)}, u32[]{:S(2)}, u32[]{:S(2)}) %collective-permute-start.22) | collective-permute-done | bytes 2336 | tf_op jit(solution)/shard_map/ppermute | solution.py:22
  200.2 5.5 collective-permute-done.23
  218.0 7.9 %collective-permute-done.28 = f32[16,6,6,1]{3,0,2,1:T(8,128)S(1)} collective-permute-done((f32[16,6,6,1]{3,0,2,1:T(8,128)S(1)}, f32[16,6,6,1]{3,0,2,1:T(8,128)S(1)}, u32[]{:S(2)}, u32[]{:S(2)}) %collective-permute-start.28) | collective-permute-done | bytes 2336 | tf_op jit(solution)/shard_map/ppermute | solution.py:22
  225.8 5.2 collective-permute-done.29
  231.6 7.5 %broadcast_in_dim.4 = f32[16,4,2,4,2,128,2]{0,6,5,4,3,2,1:T(2,128)} broadcast(f32[16,4,4,128]{0,3,2,1:T(8,128)S(1)} %copy.731), dimensions={0,1,3,5} | broadcast | bytes 1179648 | tf_op jit(solution)/shard_map/broadcast_in_dim | solution.py:82
  239.0 6.1 %copy.732 = f32[16,8,8,256]{3,2,1,0:T(8,128)} copy(f32[16,8,8,256]{0,3,2,1:T(8,128)} %bitcast.134) | data formatting | bytes 2097152 | tf_op jit(solution)/shard_map/reshape | solution.py:82
  277.5 6.5 %fusion.45 = f32[16,8,8,256]{3,2,1,0:T(8,128)S(1)} fusion(f32[16,8,8,256]{3,2,1,0:T(8,128)} %copy-done.1, f32[16,8,8,256]{3,2,1,0:T(8,128)S(1)} %get-tuple-element.32, f32[16,10,10,1]{3,2,1,0:T(8,128)} %copy.742, f32[16,10,1,256]{3,2,1,0:T(1,128)S(1)} %copy.736, f32[16,10,1,256]{3,2,1,0:T(1,128)S(1)} %copy.734, f32[16,1,8,256]{3,2,1,0:T(8,128)} %copy-done.16, ...), kind=kLoop, calls=%fused_computation.112 | loop fusion | flops 7602176 | bytes 3748352 | tf_op jit(solution)/shard_map/add | solution.py:86
  285.8 5.3 collective-permute-done.36
  294.3 9.6 %collective-permute-done.39 = f32[16,12,2,256]{3,0,2,1:T(8,128)S(1)} collective-permute-done((f32[16,12,2,256]{3,0,2,1:T(8,128)S(1)}, f32[16,12,2,256]{3,0,2,1:T(8,128)S(1)}, u32[]{:S(2)}, u32[]{:S(2)}) %collective-permute-start.39) | collective-permute-done | bytes 393248 | tf_op jit(solution)/shard_map/ppermute | solution.py:25
  304.1 8.1 %collective-permute-done.38 = f32[16,12,2,256]{3,0,2,1:T(8,128)S(1)} collective-permute-done((f32[16,12,2,256]{3,0,2,1:T(8,128)S(1)}, f32[16,12,2,256]{3,0,2,1:T(8,128)S(1)}, u32[]{:S(2)}, u32[]{:S(2)}) %collective-permute-start.38) | collective-permute-done | bytes 393248 | tf_op jit(solution)/shard_map/ppermute | solution.py:22
  332.2 8.3 %multiply_reduce_fusion = (f32[16]{0:T(128)S(1)}, f32[16]{0:T(128)S(1)}, f32[16]{0:T(128)}, f32[16]{0:T(128)}, f32[16]{0:T(128)}, /*index=5*/f32[16]{0:T(128)}, ...) fusion(f32[16,8,8,256]{3,2,1,0:T(8,128)S(1)} %fusion.45, ...), kind=kLoop, calls=%fused_computation.189 | loop fusion | flops 21495632 | bytes 6656768 | tf_op jit(solution)/shard_map/reduce_sum | solution.py:90
  341.9 39.6 %psum.15 = f32[11,16]{1,0:T(8,128)S(1)} all-reduce(f32[11,16]{1,0:T(8,128)S(1)} %stack.59), channel_id=1, replica_groups=mesh['gx'=4,'gy'=4,'gz'=2] {'gx','gy','gz'}, use_global_device_ids=true, to_apply=%region_15.0 | all-reduce | flops 176 | bytes 1408 | tf_op jit(solution)/shard_map/psum | solution.py:109
  422.2 6.0 %copy.763 = f32[16,8,8,256]{0,3,2,1:T(8,128)} copy(f32[16,8,8,256]{3,2,1,0:T(8,128)} %fusion.27) | data formatting | bytes 2097152 | tf_op jit(solution)/shard_map/sub | solution.py:75
  428.2 8.7 %reduce_sum.149 = f32[16,4,4,128]{0,3,2,1:T(8,128)S(1)} reduce(f32[16,4,2,4,2,128,2]{0,6,5,4,3,2,1:T(2,128)} %bitcast.132, f32[]{:T(128)} %constant.50.clone.1), dimensions={2,4,6}, to_apply=%region_16.0 | reduce | flops 229376 | bytes 1179652 | tf_op jit(solution)/shard_map/reduce_sum | solution.py:78
  449.8 7.9 %collective-permute-done.52 = f32[16,6,6,1]{3,0,2,1:T(8,128)S(1)} collective-permute-done((f32[16,6,6,1]{3,0,2,1:T(8,128)S(1)}, f32[16,6,6,1]{3,0,2,1:T(8,128)S(1)}, u32[]{:S(2)}, u32[]{:S(2)}) %collective-permute-start.52) | collective-permute-done | bytes 2336 | tf_op jit(solution)/shard_map/ppermute | solution.py:22
  457.7 5.5 collective-permute-done.53
  475.4 7.9 %collective-permute-done.58 = f32[16,6,6,1]{3,0,2,1:T(8,128)S(1)} collective-permute-done((f32[16,6,6,1]{3,0,2,1:T(8,128)S(1)}, f32[16,6,6,1]{3,0,2,1:T(8,128)S(1)}, u32[]{:S(2)}, u32[]{:S(2)}) %collective-permute-start.58) | collective-permute-done | bytes 2336 | tf_op jit(solution)/shard_map/ppermute | solution.py:22
  483.3 5.2 collective-permute-done.59
  501.5 7.9 %collective-permute-done.64 = f32[16,6,6,1]{3,0,2,1:T(8,128)S(1)} collective-permute-done((f32[16,6,6,1]{3,0,2,1:T(8,128)S(1)}, f32[16,6,6,1]{3,0,2,1:T(8,128)S(1)}, u32[]{:S(2)}, u32[]{:S(2)}) %collective-permute-start.64) | collective-permute-done | bytes 2336 | tf_op jit(solution)/shard_map/ppermute | solution.py:22
  509.4 5.2 collective-permute-done.65
  515.1 7.5 %broadcast_in_dim.5 = f32[16,4,2,4,2,128,2]{0,6,5,4,3,2,1:T(2,128)} broadcast(f32[16,4,4,128]{0,3,2,1:T(8,128)S(1)} %copy.767), dimensions={0,1,3,5} | broadcast | bytes 1179648 | tf_op jit(solution)/shard_map/broadcast_in_dim | solution.py:82
  522.5 6.1 %copy.768 = f32[16,8,8,256]{3,2,1,0:T(8,128)} copy(f32[16,8,8,256]{0,3,2,1:T(8,128)} %bitcast.135) | data formatting | bytes 2097152 | tf_op jit(solution)/shard_map/reshape | solution.py:82
  539.0 4.6 collective-permute-done.69
  (283 shorter events, 278.5 us)
Async XLA Ops:
  1.8 6.7 %collective-permute-start = (f32[16,2,8,256]{3,2,1,0:T(8,128)S(1)}, f32[16,2,8,256]{3,2,1,0:T(8,128)S(1)}, u32[]{:S(2)}, u32[]{:S(2)}) collective-permute-start(f32[16,2,8,256]{3,2,1,0:T(8,128)S(1)} %get-tuple-element.72), channel_id=1, source_target_pairs={{0,8},{8,16},{16,24},{24,0},{1,9},{9,17},{17,25},{25,1},{2,10},{10... | collective-permute-start | bytes 786440 | tf_op jit(solution)/shard_map/ppermute | solution.py:22
  2.3 8.6 %collective-permute-start.1 = (f32[16,2,8,256]{3,2,1,0:T(8,128)S(1)}, f32[16,2,8,256]{3,2,1,0:T(8,128)S(1)}, u32[]{:S(2)}, u32[]{:S(2)}) collective-permute-start(f32[16,2,8,256]{3,2,1,0:T(8,128)S(1)} %get-tuple-element.71), channel_id=1, source_target_pairs={{8,0},{16,8},{24,16},{0,24},{9,1},{17,9},{25,17},{1,25},{10,2},{18... | collective-permute-start | bytes 786440 | tf_op jit(solution)/shard_map/ppermute | solution.py:25
  11.4 13.3 %collective-permute-start.3 = (f32[16,12,2,256]{3,0,2,1:T(8,128)S(1)}, f32[16,12,2,256]{3,0,2,1:T(8,128)S(1)}, u32[]{:S(2)}, u32[]{:S(2)}) collective-permute-start(f32[16,12,2,256]{3,0,2,1:T(8,128)S(1)} %copy.780), channel_id=1, source_target_pairs={{2,0},{4,2},{6,4},{0,6},{3,1},{5,3},{7,5},{1,7},{10,8},{12,10},{14... | collective-permute-start | bytes 1179656 | tf_op jit(solution)/shard_map/ppermute | solution.py:25
  15.3 18.4 %collective-permute-start.2 = (f32[16,12,2,256]{3,0,2,1:T(8,128)S(1)}, f32[16,12,2,256]{3,0,2,1:T(8,128)S(1)}, u32[]{:S(2)}, u32[]{:S(2)}) collective-permute-start(f32[16,12,2,256]{3,0,2,1:T(8,128)S(1)} %copy.779), channel_id=1, source_target_pairs={{0,2},{2,4},{4,6},{6,0},{1,3},{3,5},{5,7},{7,1},{8,10},{10,12},{12... | collective-permute-start | bytes 1179656 | tf_op jit(solution)/shard_map/ppermute | solution.py:22
  107.6 6.9 %collective-permute-start.9 = (f32[16,10,1,256]{3,0,2,1:T(8,128)S(1)}, f32[16,10,1,256]{3,0,2,1:T(8,128)S(1)}, u32[]{:S(2)}, u32[]{:S(2)}) collective-permute-start(f32[16,10,1,256]{3,0,2,1:T(8,128)S(1)} %copy.719), channel_id=1, source_target_pairs={{2,0},{4,2},{6,4},{0,6},{3,1},{5,3},{7,5},{1,7},{10,8},{12,10},{14... | collective-permute-start | bytes 491528 | tf_op jit(solution)/shard_map/ppermute | solution.py:25
  109.2 9.4 %collective-permute-start.8 = (f32[16,10,1,256]{3,0,2,1:T(8,128)S(1)}, f32[16,10,1,256]{3,0,2,1:T(8,128)S(1)}, u32[]{:S(2)}, u32[]{:S(2)}) collective-permute-start(f32[16,10,1,256]{3,0,2,1:T(8,128)S(1)} %copy.717), channel_id=1, source_target_pairs={{0,2},{2,4},{4,6},{6,0},{1,3},{3,5},{5,7},{7,1},{8,10},{10,12},{12... | collective-permute-start | bytes 491528 | tf_op jit(solution)/shard_map/ppermute | solution.py:22
  163.8 9.9 %collective-permute-start.16 = (f32[16,6,6,1]{3,0,2,1:T(8,128)S(1)}, f32[16,6,6,1]{3,0,2,1:T(8,128)S(1)}, u32[]{:S(2)}, u32[]{:S(2)}) collective-permute-start(f32[16,6,6,1]{3,0,2,1:T(8,128)S(1)} %get-tuple-element.83), channel_id=1, source_target_pairs={{0,1},{1,0},{2,3},{3,2},{4,5},{5,4},{6,7},{7,6},{8,9},{9,8},{10,11... | collective-permute-start | bytes 6920 | tf_op jit(solution)/shard_map/ppermute | solution.py:22
  164.2 15.3 %collective-permute-start.17 = (f32[16,6,6,1]{3,0,2,1:T(8,128)S(1)}, f32[16,6,6,1]{3,0,2,1:T(8,128)S(1)}, u32[]{:S(2)}, u32[]{:S(2)}) collective-permute-start(f32[16,6,6,1]{3,0,2,1:T(8,128)S(1)} %get-tuple-element.84), channel_id=1, source_target_pairs={{1,0},{0,1},{3,2},{2,3},{5,4},{4,5},{7,6},{6,7},{9,8},{8,9},{11,10... | collective-permute-start | bytes 6920 | tf_op jit(solution)/shard_map/ppermute | solution.py:25
  190.2 9.9 %collective-permute-start.22 = (f32[16,6,6,1]{3,0,2,1:T(8,128)S(1)}, f32[16,6,6,1]{3,0,2,1:T(8,128)S(1)}, u32[]{:S(2)}, u32[]{:S(2)}) collective-permute-start(f32[16,6,6,1]{3,0,2,1:T(8,128)S(1)} %get-tuple-element.81), channel_id=1, source_target_pairs={{0,1},{1,0},{2,3},{3,2},{4,5},{5,4},{6,7},{7,6},{8,9},{9,8},{10,11... | collective-permute-start | bytes 6920 | tf_op jit(solution)/shard_map/ppermute | solution.py:22
  191.1 14.6 %collective-permute-start.23 = (f32[16,6,6,1]{3,0,2,1:T(8,128)S(1)}, f32[16,6,6,1]{3,0,2,1:T(8,128)S(1)}, u32[]{:S(2)}, u32[]{:S(2)}) collective-permute-start(f32[16,6,6,1]{3,0,2,1:T(8,128)S(1)} %get-tuple-element.82), channel_id=1, source_target_pairs={{1,0},{0,1},{3,2},{2,3},{5,4},{4,5},{7,6},{6,7},{9,8},{8,9},{11,10... | collective-permute-start | bytes 6920 | tf_op jit(solution)/shard_map/ppermute | solution.py:25
  209.2 6.5 %collective-permute-start.26 = (f32[16,6,1,128]{3,0,2,1:T(8,128)S(1)}, f32[16,6,1,128]{3,0,2,1:T(8,128)S(1)}, u32[]{:S(2)}, u32[]{:S(2)}) collective-permute-start(f32[16,6,1,128]{3,0,2,1:T(8,128)S(1)} %get-tuple-element.95), channel_id=1, source_target_pairs={{0,2},{2,4},{4,6},{6,0},{1,3},{3,5},{5,7},{7,1},{8,10},{10,12},{12... | collective-permute-start | bytes 147464 | tf_op jit(solution)/shard_map/ppermute | solution.py:22
  215.9 9.9 %collective-permute-start.28 = (f32[16,6,6,1]{3,0,2,1:T(8,128)S(1)}, f32[16,6,6,1]{3,0,2,1:T(8,128)S(1)}, u32[]{:S(2)}, u32[]{:S(2)}) collective-permute-start(f32[16,6,6,1]{3,0,2,1:T(8,128)S(1)} %get-tuple-element.79), channel_id=1, source_target_pairs={{0,1},{1,0},{2,3},{3,2},{4,5},{5,4},{6,7},{7,6},{8,9},{9,8},{10,11... | collective-permute-start | bytes 6920 | tf_op jit(solution)/shard_map/ppermute | solution.py:22
  216.7 14.3 %collective-permute-start.29 = (f32[16,6,6,1]{3,0,2,1:T(8,128)S(1)}, f32[16,6,6,1]{3,0,2,1:T(8,128)S(1)}, u32[]{:S(2)}, u32[]{:S(2)}) collective-permute-start(f32[16,6,6,1]{3,0,2,1:T(8,128)S(1)} %get-tuple-element.80), channel_id=1, source_target_pairs={{1,0},{0,1},{3,2},{2,3},{5,4},{4,5},{7,6},{6,7},{9,8},{8,9},{11,10... | collective-permute-start | bytes 6920 | tf_op jit(solution)/shard_map/ppermute | solution.py:25
  251.5 7.7 %collective-permute-start.33 = (f32[16,10,1,256]{3,0,2,1:T(8,128)S(1)}, f32[16,10,1,256]{3,0,2,1:T(8,128)S(1)}, u32[]{:S(2)}, u32[]{:S(2)}) collective-permute-start(f32[16,10,1,256]{3,0,2,1:T(8,128)S(1)} %copy.735), channel_id=1, source_target_pairs={{2,0},{4,2},{6,4},{0,6},{3,1},{5,3},{7,5},{1,7},{10,8},{12,10},{14... | collective-permute-start | bytes 491528 | tf_op jit(solution)/shard_map/ppermute | solution.py:25
  254.8 8.9 %collective-permute-start.32 = (f32[16,10,1,256]{3,0,2,1:T(8,128)S(1)}, f32[16,10,1,256]{3,0,2,1:T(8,128)S(1)}, u32[]{:S(2)}, u32[]{:S(2)}) collective-permute-start(f32[16,10,1,256]{3,0,2,1:T(8,128)S(1)} %copy.733), channel_id=1, source_target_pairs={{0,2},{2,4},{4,6},{6,0},{1,3},{3,5},{5,7},{7,1},{8,10},{10,12},{12... | collective-permute-start | bytes 491528 | tf_op jit(solution)/shard_map/ppermute | solution.py:22
  284.0 7.1 %collective-permute-start.36 = (f32[16,2,8,256]{3,2,1,0:T(8,128)S(1)}, f32[16,2,8,256]{3,2,1,0:T(8,128)S(1)}, u32[]{:S(2)}, u32[]{:S(2)}) collective-permute-start(f32[16,2,8,256]{3,2,1,0:T(8,128)S(1)} %get-tuple-element.62), channel_id=1, source_target_pairs={{0,8},{8,16},{16,24},{24,0},{1,9},{9,17},{17,25},{25,1},{2,10},{10... | collective-permute-start | bytes 786440 | tf_op jit(solution)/shard_map/ppermute | solution.py:22
  284.1 7.3 %collective-permute-start.37 = (f32[16,2,8,256]{3,2,1,0:T(8,128)S(1)}, f32[16,2,8,256]{3,2,1,0:T(8,128)S(1)}, u32[]{:S(2)}, u32[]{:S(2)}) collective-permute-start(f32[16,2,8,256]{3,2,1,0:T(8,128)S(1)} %get-tuple-element.63), channel_id=1, source_target_pairs={{8,0},{16,8},{24,16},{0,24},{9,1},{17,9},{25,17},{1,25},{10,2},{18... | collective-permute-start | bytes 786440 | tf_op jit(solution)/shard_map/ppermute | solution.py:25
  291.8 12.0 %collective-permute-start.39 = (f32[16,12,2,256]{3,0,2,1:T(8,128)S(1)}, f32[16,12,2,256]{3,0,2,1:T(8,128)S(1)}, u32[]{:S(2)}, u32[]{:S(2)}) collective-permute-start(f32[16,12,2,256]{3,0,2,1:T(8,128)S(1)} %copy.745), channel_id=1, source_target_pairs={{2,0},{4,2},{6,4},{0,6},{3,1},{5,3},{7,5},{1,7},{10,8},{12,10},{14... | collective-permute-start | bytes 1179656 | tf_op jit(solution)/shard_map/ppermute | solution.py:25
  293.9 18.3 %collective-permute-start.38 = (f32[16,12,2,256]{3,0,2,1:T(8,128)S(1)}, f32[16,12,2,256]{3,0,2,1:T(8,128)S(1)}, u32[]{:S(2)}, u32[]{:S(2)}) collective-permute-start(f32[16,12,2,256]{3,0,2,1:T(8,128)S(1)} %copy.743), channel_id=1, source_target_pairs={{0,2},{2,4},{4,6},{6,0},{1,3},{3,5},{5,7},{7,1},{8,10},{10,12},{12... | collective-permute-start | bytes 1179656 | tf_op jit(solution)/shard_map/ppermute | solution.py:22
  318.5 6.4 %collective-permute-start.40 = (f32[16,12,12,2]{0,3,2,1:T(2,128)}, f32[16,12,12,2]{0,3,2,1:T(2,128)}, u32[]{:S(2)}, u32[]{:S(2)}) collective-permute-start(f32[16,12,12,2]{0,3,2,1:T(2,128)} %copy.749), channel_id=1, source_target_pairs={{0,1},{1,0},{2,3},{3,2},{4,5},{5,4},{6,7},{7,6},{8,9},{9,8},{10,11... | collective-permute-start | bytes 55304 | tf_op jit(solution)/shard_map/ppermute | solution.py:22
  390.5 6.9 %collective-permute-start.45 = (f32[16,10,1,256]{3,0,2,1:T(8,128)S(1)}, f32[16,10,1,256]{3,0,2,1:T(8,128)S(1)}, u32[]{:S(2)}, u32[]{:S(2)}) collective-permute-start(f32[16,10,1,256]{3,0,2,1:T(8,128)S(1)} %copy.755), channel_id=1, source_target_pairs={{2,0},{4,2},{6,4},{0,6},{3,1},{5,3},{7,5},{1,7},{10,8},{12,10},{14... | collective-permute-start | bytes 491528 | tf_op jit(solution)/shard_map/ppermute | solution.py:25
  392.9 9.1 %collective-permute-start.44 = (f32[16,10,1,256]{3,0,2,1:T(8,128)S(1)}, f32[16,10,1,256]{3,0,2,1:T(8,128)S(1)}, u32[]{:S(2)}, u32[]{:S(2)}) collective-permute-start(f32[16,10,1,256]{3,0,2,1:T(8,128)S(1)} %copy.753), channel_id=1, source_target_pairs={{0,2},{2,4},{4,6},{6,0},{1,3},{3,5},{5,7},{7,1},{8,10},{10,12},{12... | collective-permute-start | bytes 491528 | tf_op jit(solution)/shard_map/ppermute | solution.py:22
  447.7 9.9 %collective-permute-start.52 = (f32[16,6,6,1]{3,0,2,1:T(8,128)S(1)}, f32[16,6,6,1]{3,0,2,1:T(8,128)S(1)}, u32[]{:S(2)}, u32[]{:S(2)}) collective-permute-start(f32[16,6,6,1]{3,0,2,1:T(8,128)S(1)} %get-tuple-element.77), channel_id=1, source_target_pairs={{0,1},{1,0},{2,3},{3,2},{4,5},{5,4},{6,7},{7,6},{8,9},{9,8},{10,11... | collective-permute-start | bytes 6920 | tf_op jit(solution)/shard_map/ppermute | solution.py:22
  448.2 15.0 %collective-permute-start.53 = (f32[16,6,6,1]{3,0,2,1:T(8,128)S(1)}, f32[16,6,6,1]{3,0,2,1:T(8,128)S(1)}, u32[]{:S(2)}, u32[]{:S(2)}) collective-permute-start(f32[16,6,6,1]{3,0,2,1:T(8,128)S(1)} %get-tuple-element.78), channel_id=1, source_target_pairs={{1,0},{0,1},{3,2},{2,3},{5,4},{4,5},{7,6},{6,7},{9,8},{8,9},{11,10... | collective-permute-start | bytes 6920 | tf_op jit(solution)/shard_map/ppermute | solution.py:25
  466.8 6.4 %collective-permute-start.56 = (f32[16,6,1,128]{3,0,2,1:T(8,128)S(1)}, f32[16,6,1,128]{3,0,2,1:T(8,128)S(1)}, u32[]{:S(2)}, u32[]{:S(2)}) collective-permute-start(f32[16,6,1,128]{3,0,2,1:T(8,128)S(1)} %get-tuple-element.91), channel_id=1, source_target_pairs={{0,2},{2,4},{4,6},{6,0},{1,3},{3,5},{5,7},{7,1},{8,10},{10,12},{12... | collective-permute-start | bytes 147464 | tf_op jit(solution)/shard_map/ppermute | solution.py:22
  473.4 9.9 %collective-permute-start.58 = (f32[16,6,6,1]{3,0,2,1:T(8,128)S(1)}, f32[16,6,6,1]{3,0,2,1:T(8,128)S(1)}, u32[]{:S(2)}, u32[]{:S(2)}) collective-permute-start(f32[16,6,6,1]{3,0,2,1:T(8,128)S(1)} %get-tuple-element.75), channel_id=1, source_target_pairs={{0,1},{1,0},{2,3},{3,2},{4,5},{5,4},{6,7},{7,6},{8,9},{9,8},{10,11... | collective-permute-start | bytes 6920 | tf_op jit(solution)/shard_map/ppermute | solution.py:22
  473.9 14.6 %collective-permute-start.59 = (f32[16,6,6,1]{3,0,2,1:T(8,128)S(1)}, f32[16,6,6,1]{3,0,2,1:T(8,128)S(1)}, u32[]{:S(2)}, u32[]{:S(2)}) collective-permute-start(f32[16,6,6,1]{3,0,2,1:T(8,128)S(1)} %get-tuple-element.76), channel_id=1, source_target_pairs={{1,0},{0,1},{3,2},{2,3},{5,4},{4,5},{7,6},{6,7},{9,8},{8,9},{11,10... | collective-permute-start | bytes 6920 | tf_op jit(solution)/shard_map/ppermute | solution.py:25
  492.1 6.2 %collective-permute-start.62 = (f32[16,6,1,128]{3,0,2,1:T(8,128)S(1)}, f32[16,6,1,128]{3,0,2,1:T(8,128)S(1)}, u32[]{:S(2)}, u32[]{:S(2)}) collective-permute-start(f32[16,6,1,128]{3,0,2,1:T(8,128)S(1)} %get-tuple-element.89), channel_id=1, source_target_pairs={{0,2},{2,4},{4,6},{6,0},{1,3},{3,5},{5,7},{7,1},{8,10},{10,12},{12... | collective-permute-start | bytes 147464 | tf_op jit(solution)/shard_map/ppermute | solution.py:22
  499.4 9.9 %collective-permute-start.64 = (f32[16,6,6,1]{3,0,2,1:T(8,128)S(1)}, f32[16,6,6,1]{3,0,2,1:T(8,128)S(1)}, u32[]{:S(2)}, u32[]{:S(2)}) collective-permute-start(f32[16,6,6,1]{3,0,2,1:T(8,128)S(1)} %get-tuple-element.73), channel_id=1, source_target_pairs={{0,1},{1,0},{2,3},{3,2},{4,5},{5,4},{6,7},{7,6},{8,9},{9,8},{10,11... | collective-permute-start | bytes 6920 | tf_op jit(solution)/shard_map/ppermute | solution.py:22
  499.8 14.7 %collective-permute-start.65 = (f32[16,6,6,1]{3,0,2,1:T(8,128)S(1)}, f32[16,6,6,1]{3,0,2,1:T(8,128)S(1)}, u32[]{:S(2)}, u32[]{:S(2)}) collective-permute-start(f32[16,6,6,1]{3,0,2,1:T(8,128)S(1)} %get-tuple-element.74), channel_id=1, source_target_pairs={{1,0},{0,1},{3,2},{2,3},{5,4},{4,5},{7,6},{6,7},{9,8},{8,9},{11,10... | collective-permute-start | bytes 6920 | tf_op jit(solution)/shard_map/ppermute | solution.py:25
  535.3 8.2 %collective-permute-start.69 = (f32[16,10,1,256]{3,0,2,1:T(8,128)S(1)}, f32[16,10,1,256]{3,0,2,1:T(8,128)S(1)}, u32[]{:S(2)}, u32[]{:S(2)}) collective-permute-start(f32[16,10,1,256]{3,0,2,1:T(8,128)S(1)} %copy.771), channel_id=1, source_target_pairs={{2,0},{4,2},{6,4},{0,6},{3,1},{5,3},{7,5},{1,7},{10,8},{12,10},{14... | collective-permute-start | bytes 491528 | tf_op jit(solution)/shard_map/ppermute | solution.py:25
  538.9 8.6 %collective-permute-start.68 = (f32[16,10,1,256]{3,0,2,1:T(8,128)S(1)}, f32[16,10,1,256]{3,0,2,1:T(8,128)S(1)}, u32[]{:S(2)}, u32[]{:S(2)}) collective-permute-start(f32[16,10,1,256]{3,0,2,1:T(8,128)S(1)} %copy.769), channel_id=1, source_target_pairs={{0,2},{2,4},{4,6},{6,0},{1,3},{3,5},{5,7},{7,1},{8,10},{10,12},{12... | collective-permute-start | bytes 491528 | tf_op jit(solution)/shard_map/ppermute | solution.py:22
  (58 other events, 394.5 us)
where the time goes:
time: 576 us; the launch traced here: 568 us
  waiting for transfers between devices  207 us (36%)
  local copies, waits for them, and re-layouts  125 us (22%)
  starting transfers between devices  89 us (15%)
  blocking collectives  79 us (14%)
  other arithmetic  65.7 us (11%)
    ppermute x36, waiting for transfers between devices, with_halo(): lax.ppermute(lax.slice_in_dim(block, block.shape[dim] - width, None, axis...  126 us
    ppermute x36, waiting for transfers between devices, with_halo(): lax.ppermute(lax.slice_in_dim(block, 0, width, axis=dim), axis, backward)  80.3 us
    ppermute x36, starting transfers between devices, with_halo(): lax.ppermute(lax.slice_in_dim(block, 0, width, axis=dim), axis, backward)  69.4 us
    psum x1, blocking collectives, body(): lax.psum(jnp.stack([inner_product(residual, response), inner_product(resp...  39.6 us
    psum x1, blocking collectives, body(): lax.psum(jnp.stack([inner_product(orbitals, orbitals), inner_product(orbi...  39.4 us
    slice x35, local copies, waits for them, and re-layouts, with_halo(): lax.slice_in_dim(block, block.shape[dim] - width, None, axis=dim)  27.5 us
    ppermute x36, starting transfers between devices, with_halo(): lax.ppermute(lax.slice_in_dim(block, block.shape[dim] - width, None, axis...  19.7 us
    ppermute x12, local copies, waits for them, and re-layouts, with_halo(): lax.ppermute(lax.slice_in_dim(block, 0, width, axis=dim), axis, backward)  19.1 us
  transfers between devices with their start and end apart: 72, of which 59 were waited for; matrix products, arithmetic and copies ran while one was open for 6% of the time, Pallas kernels for 0%

commit v1 on v0

--- a/solution.py
+++ b/solution.py
@@ -96,9 +96,12 @@
 
 def body(orbitals, potential):
     applied = hamiltonian(orbitals, potential)
-    first_sums = lax.psum(
-        jnp.stack([inner_product(orbitals, orbitals), inner_product(orbitals, applied)]),
-        ("gx", "gy", "gz"),
+    first_sums = jnp.sum(
+        lax.all_gather(
+            jnp.stack([inner_product(orbitals, orbitals), inner_product(orbitals, applied)]),
+            ("gx", "gy", "gz"),
+        ),
+        axis=0,
     )
     norm_orbitals = first_sums[0]
     energy = first_sums[1] / (norm_orbitals + EPSILON)

time: 576 us -> 599 us (1.040)
  blocking collectives: 79 us -> 104 us
    all_gather x0 -> x1, blocking collectives: none -> 64.1 us  [body(): lax.all_gather(jnp.stack([inner_product(orbitals, orbitals), inner_produc...]
    psum x1 -> x0, blocking collectives: 39.4 us -> none  [body(): lax.psum(jnp.stack([inner_product(orbitals, orbitals), inner_product(orbi...]
  transfers between devices with their start and end apart: 72 -> 72, of which waited for: 59 -> 57; matrix products, arithmetic and copies ran while one was open for 6% -> 6% of each run, Pallas kernels for 0% -> 0%
where the time goes in v1:
time: 599 us; the launch traced here: 591 us
  waiting for transfers between devices  205 us (34%)
  local copies, waits for them, and re-layouts  125 us (21%)
  blocking collectives  104 us (17%)
  starting transfers between devices  88.8 us (15%)
  other arithmetic  65.8 us (11%)
    ppermute x36, waiting for transfers between devices, with_halo(): lax.ppermute(lax.slice_in_dim(block, block.shape[dim] - width, None, axis...  123 us
    ppermute x36, waiting for transfers between devices, with_halo(): lax.ppermute(lax.slice_in_dim(block, 0, width, axis=dim), axis, backward)  82.8 us
    ppermute x36, starting transfers between devices, with_halo(): lax.ppermute(lax.slice_in_dim(block, 0, width, axis=dim), axis, backward)  66.2 us
    all_gather x1, blocking collectives, body(): lax.all_gather(jnp.stack([inner_product(orbitals, orbitals), inner_produc...  64.1 us
    psum x1, blocking collectives, body(): lax.psum(jnp.stack([inner_product(residual, response), inner_product(resp...  39.5 us
    slice x35, local copies, waits for them, and re-layouts, with_halo(): lax.slice_in_dim(block, block.shape[dim] - width, None, axis=dim)  27.5 us
    ppermute x36, starting transfers between devices, with_halo(): lax.ppermute(lax.slice_in_dim(block, block.shape[dim] - width, None, axis...  22.7 us
    ppermute x12, local copies, waits for them, and re-layouts, with_halo(): lax.ppermute(lax.slice_in_dim(block, 0, width, axis=dim), axis, backward)  19.1 us
  transfers between devices with their start and end apart: 72, of which 57 were waited for; matrix products, arithmetic and copies ran while one was open for 6% of the time, Pallas kernels for 0%

profile of v1, /device:TPU:0, one launch (start us, length us, event | category | flops | bytes accessed | tf_op | source)
XLA Modules:
  0.0 590.9 jit_solution(4858735988484426181)
XLA Ops:
  15.4 9.3 %collective-permute-done.3 = f32[16,12,2,256]{3,0,2,1:T(8,128)S(1)} collective-permute-done((f32[16,12,2,256]{3,0,2,1:T(8,128)S(1)}, f32[16,12,2,256]{3,0,2,1:T(8,128)S(1)}, u32[]{:S(2)}, u32[]{:S(2)}) %collective-permute-start.3) | collective-permute-done | bytes 393248 | tf_op jit(solution)/shard_map/ppermute | solution.py:25
  25.0 8.7 %collective-permute-done.2 = f32[16,12,2,256]{3,0,2,1:T(8,128)S(1)} collective-permute-done((f32[16,12,2,256]{3,0,2,1:T(8,128)S(1)}, f32[16,12,2,256]{3,0,2,1:T(8,128)S(1)}, u32[]{:S(2)}, u32[]{:S(2)}) %collective-permute-start.2) | collective-permute-done | bytes 393248 | tf_op jit(solution)/shard_map/ppermute | solution.py:22
  53.4 7.4 %multiply_reduce_fusion.12 = (f32[16]{0:T(128)S(1)}, f32[16]{0:T(128)S(1)}, f32[16,8,8,256]{3,2,1,0:T(8,128)}) fusion(f32[16,8,8,256]{3,2,1,0:T(8,128)S(1)} %copy-done, f32[8,8,256]{2,1,0:T(8,128)S(1)} %copy-done.17, f32[16,12,12,2]{3,2,1,0:T(8,128)} %copy.716, f32[16,12,2,256]{3,2,1,0:T(2,128)S(1)} %copy.710, f32[16,12,8,256]{3,2,1,0:T(8,128)S(1)} %get-tuple-element.88, ...), kind=kLoop, calls=%fused_computation.203 | loop fusion | flops 11010016 | bytes 8753280 | tf_op jit(solution)/shard_map/reduce_sum | solution.py:90
  60.8 64.1 %all-gather.1 = f32[32,2,16]{2,1,0:T(2,128)S(1)} all-gather(f32[1,2,16]{2,1,0:T(2,128)S(1)} %maximum_bitcast_fusion), channel_id=2, replica_groups=mesh['gx'=4,'gy'=4,'gz'=2] {'gx','gy','gz'}, dimensions={0}, use_global_device_ids=true | all-gather | bytes 4224 | tf_op jit(solution)/shard_map/all_gather | solution.py:100
  134.1 8.1 %collective-permute-done.9 = f32[16,10,1,256]{3,0,2,1:T(8,128)S(1)} collective-permute-done((f32[16,10,1,256]{3,0,2,1:T(8,128)S(1)}, f32[16,10,1,256]{3,0,2,1:T(8,128)S(1)}, u32[]{:S(2)}, u32[]{:S(2)}) %collective-permute-start.9) | collective-permute-done | bytes 163872 | tf_op jit(solution)/shard_map/ppermute | solution.py:25
  162.4 6.0 %copy.727 = f32[16,8,8,256]{0,3,2,1:T(8,128)} copy(f32[16,8,8,256]{3,2,1,0:T(8,128)} %fusion.53) | data formatting | bytes 2097152 | tf_op jit(solution)/shard_map/sub | solution.py:75
  168.4 8.7 %reduce_sum.147 = f32[16,4,4,128]{0,3,2,1:T(8,128)S(1)} reduce(f32[16,4,2,4,2,128,2]{0,6,5,4,3,2,1:T(2,128)} %bitcast.135, f32[]{:T(128)} %constant.50.clone.1), dimensions={2,4,6}, to_apply=%region_3.0 | reduce | flops 229376 | bytes 1179652 | tf_op jit(solution)/shard_map/reduce_sum | solution.py:78
  189.2 7.9 %collective-permute-done.16 = f32[16,6,6,1]{3,0,2,1:T(8,128)S(1)} collective-permute-done((f32[16,6,6,1]{3,0,2,1:T(8,128)S(1)}, f32[16,6,6,1]{3,0,2,1:T(8,128)S(1)}, u32[]{:S(2)}, u32[]{:S(2)}) %collective-permute-start.16) | collective-permute-done | bytes 2336 | tf_op jit(solution)/shard_map/ppermute | solution.py:22
  197.0 6.1 %collective-permute-done.17 = f32[16,6,6,1]{3,0,2,1:T(8,128)S(1)} collective-permute-done((f32[16,6,6,1]{3,0,2,1:T(8,128)S(1)}, f32[16,6,6,1]{3,0,2,1:T(8,128)S(1)}, u32[]{:S(2)}, u32[]{:S(2)}) %collective-permute-start.17) | collective-permute-done | bytes 2336 | tf_op jit(solution)/shard_map/ppermute | solution.py:25
  215.3 7.9 %collective-permute-done.22 = f32[16,6,6,1]{3,0,2,1:T(8,128)S(1)} collective-permute-done((f32[16,6,6,1]{3,0,2,1:T(8,128)S(1)}, f32[16,6,6,1]{3,0,2,1:T(8,128)S(1)}, u32[]{:S(2)}, u32[]{:S(2)}) %collective-permute-start.22) | collective-permute-done | bytes 2336 | tf_op jit(solution)/shard_map/ppermute | solution.py:22
  223.1 5.1 collective-permute-done.23
  241.2 7.9 %collective-permute-done.28 = f32[16,6,6,1]{3,0,2,1:T(8,128)S(1)} collective-permute-done((f32[16,6,6,1]{3,0,2,1:T(8,128)S(1)}, f32[16,6,6,1]{3,0,2,1:T(8,128)S(1)}, u32[]{:S(2)}, u32[]{:S(2)}) %collective-permute-start.28) | collective-permute-done | bytes 2336 | tf_op jit(solution)/shard_map/ppermute | solution.py:22
  249.0 5.0 collective-permute-done.29
  254.5 7.5 %broadcast_in_dim.4 = f32[16,4,2,4,2,128,2]{0,6,5,4,3,2,1:T(2,128)} broadcast(f32[16,4,4,128]{0,3,2,1:T(8,128)S(1)} %copy.731), dimensions={0,1,3,5} | broadcast | bytes 1179648 | tf_op jit(solution)/shard_map/broadcast_in_dim | solution.py:82
  262.0 6.1 %copy.732 = f32[16,8,8,256]{3,2,1,0:T(8,128)} copy(f32[16,8,8,256]{0,3,2,1:T(8,128)} %bitcast.136) | data formatting | bytes 2097152 | tf_op jit(solution)/shard_map/reshape | solution.py:82
  278.2 4.6 collective-permute-done.33
  300.4 6.5 %fusion.45 = f32[16,8,8,256]{3,2,1,0:T(8,128)S(1)} fusion(f32[16,8,8,256]{3,2,1,0:T(8,128)} %copy-done.1, f32[16,8,8,256]{3,2,1,0:T(8,128)S(1)} %get-tuple-element.32, f32[16,10,10,1]{3,2,1,0:T(8,128)} %copy.742, f32[16,10,1,256]{3,2,1,0:T(1,128)S(1)} %copy.736, f32[16,10,1,256]{3,2,1,0:T(1,128)S(1)} %copy.734, f32[16,1,8,256]{3,2,1,0:T(8,128)} %copy-done.16, ...), kind=kLoop, calls=%fused_computation.112 | loop fusion | flops 7602176 | bytes 3748352 | tf_op jit(solution)/shard_map/add | solution.py:86
  308.8 5.6 collective-permute-done.36
  317.7 9.5 %collective-permute-done.39 = f32[16,12,2,256]{3,0,2,1:T(8,128)S(1)} collective-permute-done((f32[16,12,2,256]{3,0,2,1:T(8,128)S(1)}, f32[16,12,2,256]{3,0,2,1:T(8,128)S(1)}, u32[]{:S(2)}, u32[]{:S(2)}) %collective-permute-start.39) | collective-permute-done | bytes 393248 | tf_op jit(solution)/shard_map/ppermute | solution.py:25
  327.5 8.2 %collective-permute-done.38 = f32[16,12,2,256]{3,0,2,1:T(8,128)S(1)} collective-permute-done((f32[16,12,2,256]{3,0,2,1:T(8,128)S(1)}, f32[16,12,2,256]{3,0,2,1:T(8,128)S(1)}, u32[]{:S(2)}, u32[]{:S(2)}) %collective-permute-start.38) | collective-permute-done | bytes 393248 | tf_op jit(solution)/shard_map/ppermute | solution.py:22
  355.3 8.3 %multiply_reduce_fusion = (f32[16]{0:T(128)S(1)}, f32[16]{0:T(128)S(1)}, f32[16]{0:T(128)}, f32[16]{0:T(128)}, f32[16]{0:T(128)}, /*index=5*/f32[16]{0:T(128)}, ...) fusion(f32[16,8,8,256]{3,2,1,0:T(8,128)S(1)} %fusion.45, ...), kind=kLoop, calls=%fused_computation.189 | loop fusion | flops 21495632 | bytes 6656768 | tf_op jit(solution)/shard_map/reduce_sum | solution.py:90
  365.0 39.5 %psum.7 = f32[11,16]{1,0:T(8,128)S(1)} all-reduce(f32[11,16]{1,0:T(8,128)S(1)} %stack.59), channel_id=1, replica_groups=mesh['gx'=4,'gy'=4,'gz'=2] {'gx','gy','gz'}, use_global_device_ids=true, to_apply=%region_15.0 | all-reduce | flops 176 | bytes 1408 | tf_op jit(solution)/shard_map/psum | solution.py:112
  445.4 6.0 %copy.763 = f32[16,8,8,256]{0,3,2,1:T(8,128)} copy(f32[16,8,8,256]{3,2,1,0:T(8,128)} %fusion.27) | data formatting | bytes 2097152 | tf_op jit(solution)/shard_map/sub | solution.py:75
  451.4 8.7 %reduce_sum.159 = f32[16,4,4,128]{0,3,2,1:T(8,128)S(1)} reduce(f32[16,4,2,4,2,128,2]{0,6,5,4,3,2,1:T(2,128)} %bitcast.134, f32[]{:T(128)} %constant.50.clone.1), dimensions={2,4,6}, to_apply=%region_16.0 | reduce | flops 229376 | bytes 1179652 | tf_op jit(solution)/shard_map/reduce_sum | solution.py:78
  473.2 7.9 %collective-permute-done.52 = f32[16,6,6,1]{3,0,2,1:T(8,128)S(1)} collective-permute-done((f32[16,6,6,1]{3,0,2,1:T(8,128)S(1)}, f32[16,6,6,1]{3,0,2,1:T(8,128)S(1)}, u32[]{:S(2)}, u32[]{:S(2)}) %collective-permute-start.52) | collective-permute-done | bytes 2336 | tf_op jit(solution)/shard_map/ppermute | solution.py:22
  481.0 5.1 collective-permute-done.53
  498.1 7.9 %collective-permute-done.58 = f32[16,6,6,1]{3,0,2,1:T(8,128)S(1)} collective-permute-done((f32[16,6,6,1]{3,0,2,1:T(8,128)S(1)}, f32[16,6,6,1]{3,0,2,1:T(8,128)S(1)}, u32[]{:S(2)}, u32[]{:S(2)}) %collective-permute-start.58) | collective-permute-done | bytes 2336 | tf_op jit(solution)/shard_map/ppermute | solution.py:22
  505.9 5.7 collective-permute-done.59
  524.5 7.9 %collective-permute-done.64 = f32[16,6,6,1]{3,0,2,1:T(8,128)S(1)} collective-permute-done((f32[16,6,6,1]{3,0,2,1:T(8,128)S(1)}, f32[16,6,6,1]{3,0,2,1:T(8,128)S(1)}, u32[]{:S(2)}, u32[]{:S(2)}) %collective-permute-start.64) | collective-permute-done | bytes 2336 | tf_op jit(solution)/shard_map/ppermute | solution.py:22
  532.4 5.5 collective-permute-done.65
  538.3 7.5 %broadcast_in_dim.5 = f32[16,4,2,4,2,128,2]{0,6,5,4,3,2,1:T(2,128)} broadcast(f32[16,4,4,128]{0,3,2,1:T(8,128)S(1)} %copy.767), dimensions={0,1,3,5} | broadcast | bytes 1179648 | tf_op jit(solution)/shard_map/broadcast_in_dim | solution.py:82
  545.8 6.1 %copy.768 = f32[16,8,8,256]{3,2,1,0:T(8,128)} copy(f32[16,8,8,256]{0,3,2,1:T(8,128)} %bitcast.137) | data formatting | bytes 2097152 | tf_op jit(solution)/shard_map/reshape | solution.py:82
  (284 shorter events, 273.1 us)
Async XLA Ops:
  1.8 6.7 %collective-permute-start = (f32[16,2,8,256]{3,2,1,0:T(8,128)S(1)}, f32[16,2,8,256]{3,2,1,0:T(8,128)S(1)}, u32[]{:S(2)}, u32[]{:S(2)}) collective-permute-start(f32[16,2,8,256]{3,2,1,0:T(8,128)S(1)} %get-tuple-element.72), channel_id=1, source_target_pairs={{0,8},{8,16},{16,24},{24,0},{1,9},{9,17},{17,25},{25,1},{2,10},{10... | collective-permute-start | bytes 786440 | tf_op jit(solution)/shard_map/ppermute | solution.py:22
  2.3 8.6 %collective-permute-start.1 = (f32[16,2,8,256]{3,2,1,0:T(8,128)S(1)}, f32[16,2,8,256]{3,2,1,0:T(8,128)S(1)}, u32[]{:S(2)}, u32[]{:S(2)}) collective-permute-start(f32[16,2,8,256]{3,2,1,0:T(8,128)S(1)} %get-tuple-element.71), channel_id=1, source_target_pairs={{8,0},{16,8},{24,16},{0,24},{9,1},{17,9},{25,17},{1,25},{10,2},{18... | collective-permute-start | bytes 786440 | tf_op jit(solution)/shard_map/ppermute | solution.py:25
  11.4 13.3 %collective-permute-start.3 = (f32[16,12,2,256]{3,0,2,1:T(8,128)S(1)}, f32[16,12,2,256]{3,0,2,1:T(8,128)S(1)}, u32[]{:S(2)}, u32[]{:S(2)}) collective-permute-start(f32[16,12,2,256]{3,0,2,1:T(8,128)S(1)} %copy.780), channel_id=1, source_target_pairs={{2,0},{4,2},{6,4},{0,6},{3,1},{5,3},{7,5},{1,7},{10,8},{12,10},{14... | collective-permute-start | bytes 1179656 | tf_op jit(solution)/shard_map/ppermute | solution.py:25
  15.3 18.4 %collective-permute-start.2 = (f32[16,12,2,256]{3,0,2,1:T(8,128)S(1)}, f32[16,12,2,256]{3,0,2,1:T(8,128)S(1)}, u32[]{:S(2)}, u32[]{:S(2)}) collective-permute-start(f32[16,12,2,256]{3,0,2,1:T(8,128)S(1)} %copy.779), channel_id=1, source_target_pairs={{0,2},{2,4},{4,6},{6,0},{1,3},{3,5},{5,7},{7,1},{8,10},{10,12},{12... | collective-permute-start | bytes 1179656 | tf_op jit(solution)/shard_map/ppermute | solution.py:22
  131.8 10.4 %collective-permute-start.9 = (f32[16,10,1,256]{3,0,2,1:T(8,128)S(1)}, f32[16,10,1,256]{3,0,2,1:T(8,128)S(1)}, u32[]{:S(2)}, u32[]{:S(2)}) collective-permute-start(f32[16,10,1,256]{3,0,2,1:T(8,128)S(1)} %copy.719), channel_id=1, source_target_pairs={{2,0},{4,2},{6,4},{0,6},{3,1},{5,3},{7,5},{1,7},{10,8},{12,10},{14... | collective-permute-start | bytes 491528 | tf_op jit(solution)/shard_map/ppermute | solution.py:25
  131.9 10.5 %collective-permute-start.8 = (f32[16,10,1,256]{3,0,2,1:T(8,128)S(1)}, f32[16,10,1,256]{3,0,2,1:T(8,128)S(1)}, u32[]{:S(2)}, u32[]{:S(2)}) collective-permute-start(f32[16,10,1,256]{3,0,2,1:T(8,128)S(1)} %copy.717), channel_id=1, source_target_pairs={{0,2},{2,4},{4,6},{6,0},{1,3},{3,5},{5,7},{7,1},{8,10},{10,12},{12... | collective-permute-start | bytes 491528 | tf_op jit(solution)/shard_map/ppermute | solution.py:22
  187.1 9.9 %collective-permute-start.16 = (f32[16,6,6,1]{3,0,2,1:T(8,128)S(1)}, f32[16,6,6,1]{3,0,2,1:T(8,128)S(1)}, u32[]{:S(2)}, u32[]{:S(2)}) collective-permute-start(f32[16,6,6,1]{3,0,2,1:T(8,128)S(1)} %get-tuple-element.83), channel_id=1, source_target_pairs={{0,1},{1,0},{2,3},{3,2},{4,5},{5,4},{6,7},{7,6},{8,9},{9,8},{10,11... | collective-permute-start | bytes 6920 | tf_op jit(solution)/shard_map/ppermute | solution.py:22
  187.9 15.2 %collective-permute-start.17 = (f32[16,6,6,1]{3,0,2,1:T(8,128)S(1)}, f32[16,6,6,1]{3,0,2,1:T(8,128)S(1)}, u32[]{:S(2)}, u32[]{:S(2)}) collective-permute-start(f32[16,6,6,1]{3,0,2,1:T(8,128)S(1)} %get-tuple-element.84), channel_id=1, source_target_pairs={{1,0},{0,1},{3,2},{2,3},{5,4},{4,5},{7,6},{6,7},{9,8},{8,9},{11,10... | collective-permute-start | bytes 6920 | tf_op jit(solution)/shard_map/ppermute | solution.py:25
  206.8 6.2 %collective-permute-start.20 = (f32[16,6,1,128]{3,0,2,1:T(8,128)S(1)}, f32[16,6,1,128]{3,0,2,1:T(8,128)S(1)}, u32[]{:S(2)}, u32[]{:S(2)}) collective-permute-start(f32[16,6,1,128]{3,0,2,1:T(8,128)S(1)} %get-tuple-element.97), channel_id=1, source_target_pairs={{0,2},{2,4},{4,6},{6,0},{1,3},{3,5},{5,7},{7,1},{8,10},{10,12},{12... | collective-permute-start | bytes 147464 | tf_op jit(solution)/shard_map/ppermute | solution.py:22
  213.2 9.9 %collective-permute-start.22 = (f32[16,6,6,1]{3,0,2,1:T(8,128)S(1)}, f32[16,6,6,1]{3,0,2,1:T(8,128)S(1)}, u32[]{:S(2)}, u32[]{:S(2)}) collective-permute-start(f32[16,6,6,1]{3,0,2,1:T(8,128)S(1)} %get-tuple-element.81), channel_id=1, source_target_pairs={{0,1},{1,0},{2,3},{3,2},{4,5},{5,4},{6,7},{7,6},{8,9},{9,8},{10,11... | collective-permute-start | bytes 6920 | tf_op jit(solution)/shard_map/ppermute | solution.py:22
  214.1 14.1 %collective-permute-start.23 = (f32[16,6,6,1]{3,0,2,1:T(8,128)S(1)}, f32[16,6,6,1]{3,0,2,1:T(8,128)S(1)}, u32[]{:S(2)}, u32[]{:S(2)}) collective-permute-start(f32[16,6,6,1]{3,0,2,1:T(8,128)S(1)} %get-tuple-element.82), channel_id=1, source_target_pairs={{1,0},{0,1},{3,2},{2,3},{5,4},{4,5},{7,6},{6,7},{9,8},{8,9},{11,10... | collective-permute-start | bytes 6920 | tf_op jit(solution)/shard_map/ppermute | solution.py:25
  231.8 6.2 %collective-permute-start.26 = (f32[16,6,1,128]{3,0,2,1:T(8,128)S(1)}, f32[16,6,1,128]{3,0,2,1:T(8,128)S(1)}, u32[]{:S(2)}, u32[]{:S(2)}) collective-permute-start(f32[16,6,1,128]{3,0,2,1:T(8,128)S(1)} %get-tuple-element.95), channel_id=1, source_target_pairs={{0,2},{2,4},{4,6},{6,0},{1,3},{3,5},{5,7},{7,1},{8,10},{10,12},{12... | collective-permute-start | bytes 147464 | tf_op jit(solution)/shard_map/ppermute | solution.py:22
  239.1 9.9 %collective-permute-start.28 = (f32[16,6,6,1]{3,0,2,1:T(8,128)S(1)}, f32[16,6,6,1]{3,0,2,1:T(8,128)S(1)}, u32[]{:S(2)}, u32[]{:S(2)}) collective-permute-start(f32[16,6,6,1]{3,0,2,1:T(8,128)S(1)} %get-tuple-element.79), channel_id=1, source_target_pairs={{0,1},{1,0},{2,3},{3,2},{4,5},{5,4},{6,7},{7,6},{8,9},{9,8},{10,11... | collective-permute-start | bytes 6920 | tf_op jit(solution)/shard_map/ppermute | solution.py:22
  240.0 14.1 %collective-permute-start.29 = (f32[16,6,6,1]{3,0,2,1:T(8,128)S(1)}, f32[16,6,6,1]{3,0,2,1:T(8,128)S(1)}, u32[]{:S(2)}, u32[]{:S(2)}) collective-permute-start(f32[16,6,6,1]{3,0,2,1:T(8,128)S(1)} %get-tuple-element.80), channel_id=1, source_target_pairs={{1,0},{0,1},{3,2},{2,3},{5,4},{4,5},{7,6},{6,7},{9,8},{8,9},{11,10... | collective-permute-start | bytes 6920 | tf_op jit(solution)/shard_map/ppermute | solution.py:25
  274.5 8.3 %collective-permute-start.33 = (f32[16,10,1,256]{3,0,2,1:T(8,128)S(1)}, f32[16,10,1,256]{3,0,2,1:T(8,128)S(1)}, u32[]{:S(2)}, u32[]{:S(2)}) collective-permute-start(f32[16,10,1,256]{3,0,2,1:T(8,128)S(1)} %copy.735), channel_id=1, source_target_pairs={{2,0},{4,2},{6,4},{0,6},{3,1},{5,3},{7,5},{1,7},{10,8},{12,10},{14... | collective-permute-start | bytes 491528 | tf_op jit(solution)/shard_map/ppermute | solution.py:25
  278.1 8.6 %collective-permute-start.32 = (f32[16,10,1,256]{3,0,2,1:T(8,128)S(1)}, f32[16,10,1,256]{3,0,2,1:T(8,128)S(1)}, u32[]{:S(2)}, u32[]{:S(2)}) collective-permute-start(f32[16,10,1,256]{3,0,2,1:T(8,128)S(1)} %copy.733), channel_id=1, source_target_pairs={{0,2},{2,4},{4,6},{6,0},{1,3},{3,5},{5,7},{7,1},{8,10},{10,12},{12... | collective-permute-start | bytes 491528 | tf_op jit(solution)/shard_map/ppermute | solution.py:22
  307.0 7.4 %collective-permute-start.36 = (f32[16,2,8,256]{3,2,1,0:T(8,128)S(1)}, f32[16,2,8,256]{3,2,1,0:T(8,128)S(1)}, u32[]{:S(2)}, u32[]{:S(2)}) collective-permute-start(f32[16,2,8,256]{3,2,1,0:T(8,128)S(1)} %get-tuple-element.62), channel_id=1, source_target_pairs={{0,8},{8,16},{16,24},{24,0},{1,9},{9,17},{17,25},{25,1},{2,10},{10... | collective-permute-start | bytes 786440 | tf_op jit(solution)/shard_map/ppermute | solution.py:22
  307.0 7.4 %collective-permute-start.37 = (f32[16,2,8,256]{3,2,1,0:T(8,128)S(1)}, f32[16,2,8,256]{3,2,1,0:T(8,128)S(1)}, u32[]{:S(2)}, u32[]{:S(2)}) collective-permute-start(f32[16,2,8,256]{3,2,1,0:T(8,128)S(1)} %get-tuple-element.63), channel_id=1, source_target_pairs={{8,0},{16,8},{24,16},{0,24},{9,1},{17,9},{25,17},{1,25},{10,2},{18... | collective-permute-start | bytes 786440 | tf_op jit(solution)/shard_map/ppermute | solution.py:25
  314.8 12.4 %collective-permute-start.39 = (f32[16,12,2,256]{3,0,2,1:T(8,128)S(1)}, f32[16,12,2,256]{3,0,2,1:T(8,128)S(1)}, u32[]{:S(2)}, u32[]{:S(2)}) collective-permute-start(f32[16,12,2,256]{3,0,2,1:T(8,128)S(1)} %copy.745), channel_id=1, source_target_pairs={{2,0},{4,2},{6,4},{0,6},{3,1},{5,3},{7,5},{1,7},{10,8},{12,10},{14... | collective-permute-start | bytes 1179656 | tf_op jit(solution)/shard_map/ppermute | solution.py:25
  317.4 18.3 %collective-permute-start.38 = (f32[16,12,2,256]{3,0,2,1:T(8,128)S(1)}, f32[16,12,2,256]{3,0,2,1:T(8,128)S(1)}, u32[]{:S(2)}, u32[]{:S(2)}) collective-permute-start(f32[16,12,2,256]{3,0,2,1:T(8,128)S(1)} %copy.743), channel_id=1, source_target_pairs={{0,2},{2,4},{4,6},{6,0},{1,3},{3,5},{5,7},{7,1},{8,10},{10,12},{12... | collective-permute-start | bytes 1179656 | tf_op jit(solution)/shard_map/ppermute | solution.py:22
  413.5 6.9 %collective-permute-start.45 = (f32[16,10,1,256]{3,0,2,1:T(8,128)S(1)}, f32[16,10,1,256]{3,0,2,1:T(8,128)S(1)}, u32[]{:S(2)}, u32[]{:S(2)}) collective-permute-start(f32[16,10,1,256]{3,0,2,1:T(8,128)S(1)} %copy.755), channel_id=1, source_target_pairs={{2,0},{4,2},{6,4},{0,6},{3,1},{5,3},{7,5},{1,7},{10,8},{12,10},{14... | collective-permute-start | bytes 491528 | tf_op jit(solution)/shard_map/ppermute | solution.py:25
  415.9 9.1 %collective-permute-start.44 = (f32[16,10,1,256]{3,0,2,1:T(8,128)S(1)}, f32[16,10,1,256]{3,0,2,1:T(8,128)S(1)}, u32[]{:S(2)}, u32[]{:S(2)}) collective-permute-start(f32[16,10,1,256]{3,0,2,1:T(8,128)S(1)} %copy.753), channel_id=1, source_target_pairs={{0,2},{2,4},{4,6},{6,0},{1,3},{3,5},{5,7},{7,1},{8,10},{10,12},{12... | collective-permute-start | bytes 491528 | tf_op jit(solution)/shard_map/ppermute | solution.py:22
  463.8 6.5 %collective-permute-start.50 = (f32[16,6,1,128]{3,0,2,1:T(8,128)S(1)}, f32[16,6,1,128]{3,0,2,1:T(8,128)S(1)}, u32[]{:S(2)}, u32[]{:S(2)}) collective-permute-start(f32[16,6,1,128]{3,0,2,1:T(8,128)S(1)} %get-tuple-element.93), channel_id=1, source_target_pairs={{0,2},{2,4},{4,6},{6,0},{1,3},{3,5},{5,7},{7,1},{8,10},{10,12},{12... | collective-permute-start | bytes 147464 | tf_op jit(solution)/shard_map/ppermute | solution.py:22
  471.1 9.9 %collective-permute-start.52 = (f32[16,6,6,1]{3,0,2,1:T(8,128)S(1)}, f32[16,6,6,1]{3,0,2,1:T(8,128)S(1)}, u32[]{:S(2)}, u32[]{:S(2)}) collective-permute-start(f32[16,6,6,1]{3,0,2,1:T(8,128)S(1)} %get-tuple-element.77), channel_id=1, source_target_pairs={{0,1},{1,0},{2,3},{3,2},{4,5},{5,4},{6,7},{7,6},{8,9},{9,8},{10,11... | collective-permute-start | bytes 6920 | tf_op jit(solution)/shard_map/ppermute | solution.py:22
  471.5 14.6 %collective-permute-start.53 = (f32[16,6,6,1]{3,0,2,1:T(8,128)S(1)}, f32[16,6,6,1]{3,0,2,1:T(8,128)S(1)}, u32[]{:S(2)}, u32[]{:S(2)}) collective-permute-start(f32[16,6,6,1]{3,0,2,1:T(8,128)S(1)} %get-tuple-element.78), channel_id=1, source_target_pairs={{1,0},{0,1},{3,2},{2,3},{5,4},{4,5},{7,6},{6,7},{9,8},{8,9},{11,10... | collective-permute-start | bytes 6920 | tf_op jit(solution)/shard_map/ppermute | solution.py:25
  496.0 9.9 %collective-permute-start.58 = (f32[16,6,6,1]{3,0,2,1:T(8,128)S(1)}, f32[16,6,6,1]{3,0,2,1:T(8,128)S(1)}, u32[]{:S(2)}, u32[]{:S(2)}) collective-permute-start(f32[16,6,6,1]{3,0,2,1:T(8,128)S(1)} %get-tuple-element.75), channel_id=1, source_target_pairs={{0,1},{1,0},{2,3},{3,2},{4,5},{5,4},{6,7},{7,6},{8,9},{9,8},{10,11... | collective-permute-start | bytes 6920 | tf_op jit(solution)/shard_map/ppermute | solution.py:22
  497.4 14.2 %collective-permute-start.59 = (f32[16,6,6,1]{3,0,2,1:T(8,128)S(1)}, f32[16,6,6,1]{3,0,2,1:T(8,128)S(1)}, u32[]{:S(2)}, u32[]{:S(2)}) collective-permute-start(f32[16,6,6,1]{3,0,2,1:T(8,128)S(1)} %get-tuple-element.76), channel_id=1, source_target_pairs={{1,0},{0,1},{3,2},{2,3},{5,4},{4,5},{7,6},{6,7},{9,8},{8,9},{11,10... | collective-permute-start | bytes 6920 | tf_op jit(solution)/shard_map/ppermute | solution.py:25
  515.2 6.3 %collective-permute-start.62 = (f32[16,6,1,128]{3,0,2,1:T(8,128)S(1)}, f32[16,6,1,128]{3,0,2,1:T(8,128)S(1)}, u32[]{:S(2)}, u32[]{:S(2)}) collective-permute-start(f32[16,6,1,128]{3,0,2,1:T(8,128)S(1)} %get-tuple-element.89), channel_id=1, source_target_pairs={{0,2},{2,4},{4,6},{6,0},{1,3},{3,5},{5,7},{7,1},{8,10},{10,12},{12... | collective-permute-start | bytes 147464 | tf_op jit(solution)/shard_map/ppermute | solution.py:22
  522.4 9.9 %collective-permute-start.64 = (f32[16,6,6,1]{3,0,2,1:T(8,128)S(1)}, f32[16,6,6,1]{3,0,2,1:T(8,128)S(1)}, u32[]{:S(2)}, u32[]{:S(2)}) collective-permute-start(f32[16,6,6,1]{3,0,2,1:T(8,128)S(1)} %get-tuple-element.73), channel_id=1, source_target_pairs={{0,1},{1,0},{2,3},{3,2},{4,5},{5,4},{6,7},{7,6},{8,9},{9,8},{10,11... | collective-permute-start | bytes 6920 | tf_op jit(solution)/shard_map/ppermute | solution.py:22
  523.1 14.7 %collective-permute-start.65 = (f32[16,6,6,1]{3,0,2,1:T(8,128)S(1)}, f32[16,6,6,1]{3,0,2,1:T(8,128)S(1)}, u32[]{:S(2)}, u32[]{:S(2)}) collective-permute-start(f32[16,6,6,1]{3,0,2,1:T(8,128)S(1)} %get-tuple-element.74), channel_id=1, source_target_pairs={{1,0},{0,1},{3,2},{2,3},{5,4},{4,5},{7,6},{6,7},{9,8},{8,9},{11,10... | collective-permute-start | bytes 6920 | tf_op jit(solution)/shard_map/ppermute | solution.py:25
  559.0 7.0 %collective-permute-start.69 = (f32[16,10,1,256]{3,0,2,1:T(8,128)S(1)}, f32[16,10,1,256]{3,0,2,1:T(8,128)S(1)}, u32[]{:S(2)}, u32[]{:S(2)}) collective-permute-start(f32[16,10,1,256]{3,0,2,1:T(8,128)S(1)} %copy.771), channel_id=1, source_target_pairs={{2,0},{4,2},{6,4},{0,6},{3,1},{5,3},{7,5},{1,7},{10,8},{12,10},{14... | collective-permute-start | bytes 491528 | tf_op jit(solution)/shard_map/ppermute | solution.py:25
  561.6 8.9 %collective-permute-start.68 = (f32[16,10,1,256]{3,0,2,1:T(8,128)S(1)}, f32[16,10,1,256]{3,0,2,1:T(8,128)S(1)}, u32[]{:S(2)}, u32[]{:S(2)}) collective-permute-start(f32[16,10,1,256]{3,0,2,1:T(8,128)S(1)} %copy.769), channel_id=1, source_target_pairs={{0,2},{2,4},{4,6},{6,0},{1,3},{3,5},{5,7},{7,1},{8,10},{10,12},{12... | collective-permute-start | bytes 491528 | tf_op jit(solution)/shard_map/ppermute | solution.py:22
  (58 other events, 391.7 us)
